TPU v7x, 32 devices: a whole 2x2x4 slice. The times are simulated.
32 devices in a mesh: replica: 8 (over z, y), shard: 4 (over x, core).
Axes of the slice: x: 2, y: 2, z: 4, core: 2. Of those that a mesh axis runs over, the one named last changes fastest.
Arguments:
- outer_params: float32 [512, 4096], P('shard'), may hold values from -6 to 6, as said below
- local_params: bfloat16 [8, 512, 4096], P('replica', 'shard'), may hold values from -70 to 70
- momentum: float32 [512, 4096], P('shard'), may hold values from -6 to 6
Outputs:
- params_next: float32 [512, 4096], P('shard')
- momentum_next: float32 [512, 4096], P('shard')
- block_scales: float32 [32, 512], P(None, 'shard')
Inputs may be any that keep to these rules, and one draw needn't show every extreme that they name: `outer_params`: outer parameters of order one.
All inputs are finite; a program needn't handle non-finite values.
Results may differ from a plain program's by a relative error of at most 0.005.
Values may be sent and summed in bfloat16 or wider, within the bound.
A program may use at most 64 MiB of HBM per device.

v0:
```python
import math
import jax
import jax.numpy as jnp
from jax import lax
from jax.sharding import PartitionSpec as P

BLOCK = 128
epsilon = 1e-06
clip_level = 0.5
outer_rate = 0.7
outer_decay = 0.9
grid_levels = 7.0


def smooth_step(values):
    return values - jnp.sin(2.0 * math.pi * values) / (2.0 * math.pi)


def smooth_round(values):
    return smooth_step(smooth_step(values))


def block_max(values):
    return jnp.max(
        jnp.abs(values).reshape(values.shape[0], values.shape[1] // BLOCK, BLOCK), axis=2
    )


def per_device(outer_params, local_params, momentum):
    workers = lax.axis_size("replica")
    row_count = outer_params.shape[0]
    col_count = outer_params.shape[1]
    slice_rows = row_count // workers
    slice_start = lax.axis_index("replica") * slice_rows
    deltas = outer_params - local_params[0].astype(jnp.float32)
    absmax = lax.pmax(block_max(deltas), "replica")
    spread_scale = jnp.repeat(absmax + epsilon, BLOCK, axis=1)
    encoded = smooth_round(grid_levels * deltas / spread_scale).astype(jnp.bfloat16)
    arrived = lax.all_to_all(encoded[None], "replica", split_axis=1, concat_axis=0, tiled=True)
    slice_scale = lax.dynamic_slice_in_dim(spread_scale, slice_start, slice_rows, 0)
    summed_rows = jnp.sum(arrived.astype(jnp.float32), axis=0) * slice_scale / grid_levels
    gradient_slice = summed_rows / workers
    square_total = lax.psum(jnp.sum(gradient_slice * gradient_slice), ("replica", "shard"))
    entry_count = row_count * lax.axis_size("shard") * col_count
    root_mean = jnp.sqrt(square_total / entry_count + epsilon)
    factor = jnp.minimum(1.0, clip_level / root_mean)
    gradient = lax.all_gather(gradient_slice, "replica", axis=0, tiled=True)
    clipped = factor * gradient
    momentum_next = outer_decay * momentum + clipped
    params_next = outer_params - outer_rate * (clipped + outer_decay * momentum_next)
    return (params_next, momentum_next, absmax.T)


def solution(mesh):
    return jax.shard_map(
        per_device,
        mesh=mesh,
        in_specs=(P("shard", None), P("replica", "shard", None), P("shard", None)),
        out_specs=(P("shard", None), P("shard", None), P(None, "shard")),
        check_vma=False,
    )
```

profile of v0, /device:TPU:0, one launch (start us, length us, event | category | flops | bytes accessed | tf_op | source)
XLA Modules:
  0.0 172.0 jit_solution(18044409390670645208)
XLA Ops:
  7.2 2.1 %abs_bitcast_fusion = f32[16,8,32,128]{3,1,2,0:T(8,128)S(1)} fusion(f32[128,4096]{1,0:T(8,128)} %param.3, bf16[1,128,4096]{2,1,0:T(8,128)(2,1)} %param.4), kind=kLoop, calls=%fused_computation.5 | loop fusion | flops 1572864 | bytes 5242880
  9.3 0.4 copy.11
  9.7 0.0 copy-start.1
  9.7 0.6 reduce_max.9
  10.3 39.3 %pmax.7 = f32[128,32]{1,0:T(8,128)S(1)} all-reduce(f32[128,32]{1,0:T(8,128)S(1)} %reduce_max.9), channel_id=1, replica_groups=mesh['replica'=8,'shard'=4] {'replica'}, use_global_device_ids=true, to_apply=%region_1.0 | all-reduce | flops 4096 | bytes 32768 | tf_op jit(solution)/shard_map/pmax | solution.py:36
  49.6 0.6 broadcast_in_dim.6
  50.2 0.0 copy-done.1
  50.2 15.9 %fusion = bf16[1,128,4096]{2,1,0:T(8,128)(2,1)S(1)} fusion(f32[128,4096]{1,0:T(8,128)} %param.3, bf16[1,128,4096]{2,1,0:T(8,128)(2,1)S(1)} %copy-done.1, f32[16,8,32,128]{3,2,1,0:T(8,128)S(1)} %bitcast.23), kind=kLoop, calls=%fused_computation.6 | loop fusion | flops 5767168 | bytes 6291456 | tf_op jit(solution)/shard_map/broadcast_in_dim | solution.py:39
  66.1 3.7 %copy.18 = bf16[1,128,4096]{2,0,1:T(2,128)(2,1)} copy(bf16[1,128,4096]{2,1,0:T(8,128)(2,1)S(1)} %fusion) | data formatting | bytes 2097152 | tf_op jit(solution)/shard_map/broadcast_in_dim | solution.py:39
  69.8 0.5 broadcast.25
  70.3 8.4 %reduce = bf16[128,4096]{1,0:T(8,128)(2,1)S(1)} reduce(bf16[128,1,4096]{2,1,0:T(2,128)(2,1)} %bitcast.26, bf16[]{:T(256)} %broadcast.25), dimensions={1}, to_apply=%bitcast.22.reduce_sub_computation | reduce | bytes 2097154
  78.7 1.6 reshape.23
  80.3 3.6 %all-to-all-start = ((bf16[8,2,32768]{2,1,0:T(2,128)(2,1)}), bf16[8,2,32768]{2,1,0:T(2,128)(2,1)S(1)}, u32[]{:S(2)}, u32[]{:S(2)}) async-start(bf16[8,2,32768]{2,1,0:T(2,128)(2,1)} %reshape.23), calls=%async_computation | async-start | bytes 2097152 | tf_op jit(solution)/shard_map/all_to_all | solution.py:39
  83.8 0.2 all-gather.2.cloned.1.call-start
  84.1 3.0 %copy.17 = f32[16,8,32,128]{3,1,2,0:T(8,128)} copy(f32[16,8,32,128]{3,2,1,0:T(8,128)S(1)} %bitcast.24) | data formatting | bytes 4194304
  87.0 15.8 %all-to-all-done = bf16[8,2,32768]{2,1,0:T(2,128)(2,1)S(1)} async-done(((bf16[8,2,32768]{2,1,0:T(2,128)(2,1)}), bf16[8,2,32768]{2,1,0:T(2,128)(2,1)S(1)}, u32[]{:S(2)}, u32[]{:S(2)}) %all-to-all-start) | async-done | bytes 1048608 | tf_op jit(solution)/shard_map/all_to_all | solution.py:39
  102.8 1.0 reshape.24
  103.8 3.0 %copy.10 = f32[1,128,4096]{2,1,0:T(8,128)} copy(bf16[1,128,4096]{2,0,1:T(2,128)(2,1)S(1)} %bitcast.28) | data formatting | bytes 3145728
  106.8 0.0 copy-start
  106.8 1.9 %reduce_sum.18 = f32[16,4096]{1,0:T(8,128)S(1)} reduce(f32[8,16,4096]{2,1,0:T(8,128)} %bitcast.25, f32[]{:T(128)} %constant.13.clone.1), dimensions={0}, to_apply=%region_2.0 | reduce | flops 458752 | bytes 2359300 | tf_op jit(solution)/shard_map/reduce_sum | solution.py:41
  108.7 2.3 %multiply_reduce_fusion = (f32[]{:T(128)}, f32[16,4096]{1,0:T(8,128)}) fusion(f32[16,4096]{1,0:T(8,128)S(1)} %reduce_sum.18, f32[128,4096]{1,0:T(8,128)} %bitcast.29, s32[]{:T(128)S(6)} %select_n.3), kind=kLoop, calls=%fused_computation.7 | loop fusion | flops 262143 | bytes 786440 | tf_op jit(solution)/shard_map/reduce_sum | solution.py:43
  111.0 0.0 all-gather.2.cloned.1.call-update
  111.0 0.7 copy.9
  111.7 39.4 %psum.7 = f32[]{:T(128)} all-reduce(f32[]{:T(128)} %get-tuple-element.11), channel_id=1, replica_groups=mesh['replica'=8,'shard'=4] {'replica','shard'}, use_global_device_ids=true, to_apply=%region_4.0 | all-reduce | flops 1 | bytes 8 | tf_op jit(solution)/shard_map/psum | solution.py:43
  151.7 8.5 %all-gather.2.cloned.1.call-done = f32[128,4096]{1,0:T(8,128)} async-done(((f32[16,4096]{1,0:T(8,128)}), f32[128,4096]{1,0:T(8,128)}) %all-gather.2.cloned.1.call-update) | async-done | bytes 2097168 | tf_op jit(solution)/shard_map/all_gather | solution.py:47
  160.2 0.0 copy-done
  160.2 4.9 %multiply_subtract_fusion = (f32[128,4096]{1,0:T(8,128)}, f32[128,4096]{1,0:T(8,128)}) fusion(f32[128,4096]{1,0:T(8,128)S(1)} %copy-done, f32[128,4096]{1,0:T(8,128)} %all-gather.2.cloned.1.call-done, f32[]{:T(128)S(6)} %min_shard_map.3, f32[128,4096]{1,0:T(8,128)} %param.5), kind=kLoop, calls=%fused_computation.2 | loop fusion | flops 3670016 | bytes 10485764 | tf_op jit(solution)/shard_map/sub | solution.py:50
  (1 shorter events, 0.0 us)
Async XLA Ops:
  9.7 40.6 %copy-start.1 = (bf16[1,128,4096]{2,1,0:T(8,128)(2,1)S(1)}, bf16[1,128,4096]{2,1,0:T(8,128)(2,1)}, u32[]{:S(2)}) copy-start(bf16[1,128,4096]{2,1,0:T(8,128)(2,1)} %param.4) | copy-start | bytes 3145732
  80.3 22.5 %all-to-all-start = ((bf16[8,2,32768]{2,1,0:T(2,128)(2,1)}), bf16[8,2,32768]{2,1,0:T(2,128)(2,1)S(1)}, u32[]{:S(2)}, u32[]{:S(2)}) async-start(bf16[8,2,32768]{2,1,0:T(2,128)(2,1)} %reshape.23), calls=%async_computation | async-start | bytes 2097152 | tf_op jit(solution)/shard_map/all_to_all | solution.py:39
  83.8 76.4 %all-gather.2.cloned.1.call-start = ((), (), s32[]{:S(2)}) async-start(), calls=%async_computation.1 | async-start | bytes 2359296 | tf_op jit(solution)/shard_map/all_gather | solution.py:47
  106.8 53.4 %copy-start = (f32[128,4096]{1,0:T(8,128)S(1)}, f32[128,4096]{1,0:T(8,128)}, u32[]{:S(2)}) copy-start(f32[128,4096]{1,0:T(8,128)} %param.3) | copy-start | bytes 6291460
Sparse Core Ops, SparseCore 0:
  111.1 49.0 all-gather.1
where the time goes:
time: 172 us
  blocking collectives  78.7 us (46%)
  other arithmetic  36 us (21%)
  waiting for transfers between devices  24.3 us (14%)
  between operations  14.8 us (9%)
  local copies, waits for them, and re-layouts  14.4 us (8%)
  starting transfers between devices  3.78 us (2%)
    psum x1, blocking collectives, per_device(): lax.psum(jnp.sum(gradient_slice * gradient_slice), ('replica', 'shard'))  39.4 us
    pmax x1, blocking collectives, per_device(): absmax = lax.pmax(block_max(deltas), 'replica')  39.3 us
    broadcast_in_dim x1, other arithmetic, per_device(): encoded[None]  15.9 us
    all_to_all x1, waiting for transfers between devices, per_device(): lax.all_to_all(encoded[None], 'replica', split_axis=1, concat_axis=0, til...  15.8 us
    unnamed x2, other arithmetic  10.5 us
    unnamed x11, local copies, waits for them, and re-layouts  10.1 us
    all_gather x1, waiting for transfers between devices, per_device(): gradient = lax.all_gather(gradient_slice, 'replica', axis=0, tiled=True)  8.49 us
    sub x1, other arithmetic, per_device(): outer_params - outer_rate * (clipped + outer_decay * momentum_next)  4.9 us
  transfers between devices with their start and end apart: 2, of which 2 were waited for; matrix products, arithmetic and copies ran while one was open for 2% of the time, Pallas kernels for 0%

commit v1 on v0

--- a/solution.py
+++ b/solution.py
@@ -36,7 +36,15 @@
     absmax = lax.pmax(block_max(deltas), "replica")
     spread_scale = jnp.repeat(absmax + epsilon, BLOCK, axis=1)
     encoded = smooth_round(grid_levels * deltas / spread_scale).astype(jnp.bfloat16)
-    arrived = lax.all_to_all(encoded[None], "replica", split_axis=1, concat_axis=0, tiled=True)
+    arrived = jnp.concatenate(
+        lax.all_to_all(
+            jnp.stack(jnp.split(encoded[None], lax.axis_size("replica"), axis=1), 0),
+            "replica",
+            0,
+            0,
+        ),
+        axis=0,
+    )
     slice_scale = lax.dynamic_slice_in_dim(spread_scale, slice_start, slice_rows, 0)
     summed_rows = jnp.sum(arrived.astype(jnp.float32), axis=0) * slice_scale / grid_levels
     gradient_slice = summed_rows / workers

time: 172 us -> 158 us (0.919)
  other arithmetic: 36 us -> 25.9 us
  local copies, waits for them, and re-layouts: 14.4 us -> 9.93 us
    unnamed x2 -> x1, other arithmetic: 10.5 us -> 2.11 us
    broadcast_in_dim x1 -> x0, local copies, waits for them, and re-layouts: 3.68 us -> none  [per_device(): encoded[None]]
    reduce_sum x1, other arithmetic: 1.86 us -> 0.14 us  [per_device(): jnp.sum(arrived.astype(jnp.float32), axis=0) * slice_scale / grid_levels]
    unnamed x11 -> x14, local copies, waits for them, and re-layouts: 10.1 us -> 8.66 us
where the time goes in v1:
time: 158 us; the launch traced here: 157 us
  blocking collectives  78.7 us (50%)
  other arithmetic  25.9 us (16%)
  waiting for transfers between devices  24.5 us (16%)
  between operations  14.8 us (9%)
  local copies, waits for them, and re-layouts  9.93 us (6%)
  starting transfers between devices  3.6 us (2%)
    psum x1, blocking collectives, per_device(): lax.psum(jnp.sum(gradient_slice * gradient_slice), ('replica', 'shard'))  39.4 us
    pmax x1, blocking collectives, per_device(): absmax = lax.pmax(block_max(deltas), 'replica')  39.3 us
    all_to_all x1, waiting for transfers between devices, per_device(): lax.all_to_all(jnp.stack(jnp.split(encoded[None], lax.axis_size('replica'...  16 us
    broadcast_in_dim x1, other arithmetic, per_device(): encoded[None]  15.9 us
    unnamed x14, local copies, waits for them, and re-layouts  8.66 us
    all_gather x1, waiting for transfers between devices, per_device(): gradient = lax.all_gather(gradient_slice, 'replica', axis=0, tiled=True)  8.49 us
    sub x1, other arithmetic, per_device(): outer_params - outer_rate * (clipped + outer_decay * momentum_next)  4.9 us
    all_to_all x1, starting transfers between devices, per_device(): lax.all_to_all(jnp.stack(jnp.split(encoded[None], lax.axis_size('replica'...  3.56 us
  transfers between devices with their start and end apart: 2, of which 2 were waited for; matrix products, arithmetic and copies ran while one was open for 2% of the time, Pallas kernels for 0%

profile of v1, /device:TPU:0, one launch (start us, length us, event | category | flops | bytes accessed | tf_op | source)
XLA Modules:
  0.0 157.4 jit_solution(7219774458395003367)
XLA Ops:
  7.2 2.1 %abs_bitcast_fusion = f32[16,8,32,128]{3,1,2,0:T(8,128)S(1)} fusion(f32[128,4096]{1,0:T(8,128)} %param.3, bf16[1,128,4096]{2,1,0:T(8,128)(2,1)} %param.4), kind=kLoop, calls=%fused_computation.6 | loop fusion | flops 1572864 | bytes 5242880
  9.3 0.4 copy.8
  9.7 0.0 copy-start.1
  9.7 0.6 reduce_max.9
  10.3 39.3 %pmax.7 = f32[128,32]{1,0:T(8,128)S(1)} all-reduce(f32[128,32]{1,0:T(8,128)S(1)} %reduce_max.9), channel_id=1, replica_groups=mesh['replica'=8,'shard'=4] {'replica'}, use_global_device_ids=true, to_apply=%region_1.0 | all-reduce | flops 4096 | bytes 32768 | tf_op jit(solution)/shard_map/pmax | solution.py:36
  49.6 0.6 broadcast_in_dim.6
  50.2 0.0 copy-done.1
  50.2 15.9 %fusion = bf16[1,128,4096]{2,1,0:T(8,128)(2,1)S(1)} fusion(f32[128,4096]{1,0:T(8,128)} %param.3, bf16[1,128,4096]{2,1,0:T(8,128)(2,1)S(1)} %copy-done.1, f32[16,8,32,128]{3,2,1,0:T(8,128)S(1)} %bitcast.50), kind=kLoop, calls=%fused_computation.7 | loop fusion | flops 5767168 | bytes 6291456 | tf_op jit(solution)/shard_map/broadcast_in_dim | solution.py:41
  66.1 0.7 fusion.8
  66.8 0.7 fusion.7
  67.4 0.7 fusion.6
  68.1 0.7 fusion.5
  68.8 0.7 fusion.4
  69.4 0.7 fusion.3
  70.1 0.7 fusion.2
  70.8 0.7 fusion.1
  71.4 3.6 %all-to-all-start = ((bf16[8,1,16,4096]{3,2,1,0:T(8,128)(2,1)}), bf16[8,1,16,4096]{3,2,1,0:T(8,128)(2,1)S(1)}, u32[]{:S(2)}, u32[]{:S(2)}) async-start(bf16[8,1,16,4096]{3,2,1,0:T(8,128)(2,1)} %fusion.1), calls=%async_computation | async-start | bytes 2097152 | tf_op jit(solution)/shard_map/all_to_all | solution.py:40
  75.0 0.0 all-gather.2.cloned.1.call-start
  75.0 3.0 %copy.13 = f32[16,8,32,128]{3,1,2,0:T(8,128)} copy(f32[16,8,32,128]{3,2,1,0:T(8,128)S(1)} %bitcast.51) | data formatting | bytes 4194304
  78.0 0.0 copy-start
  78.0 16.0 %all-to-all-done = bf16[8,1,16,4096]{3,2,1,0:T(8,128)(2,1)S(1)} async-done(((bf16[8,1,16,4096]{3,2,1,0:T(8,128)(2,1)}), bf16[8,1,16,4096]{3,2,1,0:T(8,128)(2,1)S(1)}, u32[]{:S(2)}, u32[]{:S(2)}) %all-to-all-start) | async-done | bytes 1048608 | tf_op jit(solution)/shard_map/all_to_all | solution.py:40
  94.0 0.1 convert_reduce_fusion
  94.1 2.3 %multiply_reduce_fusion = (f32[]{:T(128)}, f32[16,4096]{1,0:T(8,128)}) fusion(f32[16,4096]{1,0:T(8,128)S(1)} %convert_reduce_fusion, f32[128,4096]{1,0:T(8,128)} %bitcast.53, s32[]{:T(128)S(6)} %select_n.3), kind=kLoop, calls=%fused_computation.8 | loop fusion | flops 262143 | bytes 786440 | tf_op jit(solution)/shard_map/reduce_sum | solution.py:51
  96.4 0.0 all-gather.2.cloned.1.call-update
  96.4 0.7 copy.7
  97.1 39.4 %psum.7 = f32[]{:T(128)} all-reduce(f32[]{:T(128)} %get-tuple-element.8), channel_id=1, replica_groups=mesh['replica'=8,'shard'=4] {'replica','shard'}, use_global_device_ids=true, to_apply=%region_4.0 | all-reduce | flops 1 | bytes 8 | tf_op jit(solution)/shard_map/psum | solution.py:51
  137.1 8.5 %all-gather.2.cloned.1.call-done = f32[128,4096]{1,0:T(8,128)} async-done(((f32[16,4096]{1,0:T(8,128)}), f32[128,4096]{1,0:T(8,128)}) %all-gather.2.cloned.1.call-update) | async-done | bytes 2097168 | tf_op jit(solution)/shard_map/all_gather | solution.py:55
  145.6 0.0 copy-done
  145.6 4.9 %multiply_subtract_fusion = (f32[128,4096]{1,0:T(8,128)}, f32[128,4096]{1,0:T(8,128)}) fusion(f32[128,4096]{1,0:T(8,128)S(1)} %copy-done, f32[128,4096]{1,0:T(8,128)} %all-gather.2.cloned.1.call-done, f32[]{:T(128)S(6)} %min_shard_map.3, f32[128,4096]{1,0:T(8,128)} %param.5), kind=kLoop, calls=%fused_computation.2 | loop fusion | flops 3670016 | bytes 10485764 | tf_op jit(solution)/shard_map/sub | solution.py:58
  (1 shorter events, 0.0 us)
Async XLA Ops:
  9.7 40.6 %copy-start.1 = (bf16[1,128,4096]{2,1,0:T(8,128)(2,1)S(1)}, bf16[1,128,4096]{2,1,0:T(8,128)(2,1)}, u32[]{:S(2)}) copy-start(bf16[1,128,4096]{2,1,0:T(8,128)(2,1)} %param.4) | copy-start | bytes 3145732
  71.4 22.5 %all-to-all-start = ((bf16[8,1,16,4096]{3,2,1,0:T(8,128)(2,1)}), bf16[8,1,16,4096]{3,2,1,0:T(8,128)(2,1)S(1)}, u32[]{:S(2)}, u32[]{:S(2)}) async-start(bf16[8,1,16,4096]{3,2,1,0:T(8,128)(2,1)} %fusion.1), calls=%async_computation | async-start | bytes 2097152 | tf_op jit(solution)/shard_map/all_to_all | solution.py:40
  75.0 70.6 %all-gather.2.cloned.1.call-start = ((), (), s32[]{:S(2)}) async-start(), calls=%async_computation.1 | async-start | bytes 2359296 | tf_op jit(solution)/shard_map/all_gather | solution.py:55
  78.0 67.6 %copy-start = (f32[128,4096]{1,0:T(8,128)S(1)}, f32[128,4096]{1,0:T(8,128)}, u32[]{:S(2)}) copy-start(f32[128,4096]{1,0:T(8,128)} %param.3) | copy-start | bytes 6291460
Sparse Core Ops, SparseCore 0:
  96.5 49.0 all-gather.1

commit v2 on v0

--- a/solution.py
+++ b/solution.py
@@ -10,6 +10,15 @@
 outer_rate = 0.7
 outer_decay = 0.9
 grid_levels = 7.0
+
+
+def get_ports(a0):
+    return jnp.concatenate(
+        jax.lax.all_to_all(
+            jnp.stack([a0 for _ in range(jax.lax.axis_size("replica"))]), "replica", 0, 0
+        ),
+        0,
+    )
 
 
 def smooth_step(values):
@@ -44,7 +53,7 @@
     entry_count = row_count * lax.axis_size("shard") * col_count
     root_mean = jnp.sqrt(square_total / entry_count + epsilon)
     factor = jnp.minimum(1.0, clip_level / root_mean)
-    gradient = lax.all_gather(gradient_slice, "replica", axis=0, tiled=True)
+    gradient = get_ports(gradient_slice)
     clipped = factor * gradient
     momentum_next = outer_decay * momentum + clipped
     params_next = outer_params - outer_rate * (clipped + outer_decay * momentum_next)

time: 172 us -> 188 us (1.093)
  blocking collectives: 78.7 us -> 104 us
  between operations: 14.8 us -> 1.43 us
  waiting for transfers between devices: 24.3 us -> 14 us
  local copies, waits for them, and re-layouts: 14.4 us -> 24.5 us
  starting transfers between devices: 3.78 us -> 8.08 us
    psum x1, blocking collectives: 39.4 us -> 64.2 us  [per_device(): lax.psum(jnp.sum(gradient_slice * gradient_slice), ('replica', 'shard'))]
    unnamed x11 -> x15, local copies, waits for them, and re-layouts: 10.1 us -> 18.7 us
    all_gather x1 -> x0, waiting for transfers between devices: 8.49 us -> none  [per_device(): gradient = lax.all_gather(gradient_slice, 'replica', axis=0, tiled=True)]
    all_to_all x0 -> x1, starting transfers between devices: none -> 4.34 us  [get_ports(): jax.lax.all_to_all(jnp.stack([a0 for _ in range(jax.lax.axis_size('replic...]
    sub x1, other arithmetic: 4.9 us -> 2.84 us  [per_device(): outer_params - outer_rate * (clipped + outer_decay * momentum_next)]
    mul x0 -> x1, other arithmetic: none -> 1.91 us  [per_device(): clipped = factor * gradient]
  transfers between devices with their start and end apart: 2 -> 2, of which waited for: 2 -> 1; matrix products, arithmetic and copies ran while one was open for 2% -> 3% of each run, Pallas kernels for 0% -> 0%
where the time goes in v2:
time: 188 us; the launch traced here: 187 us
  blocking collectives  104 us (55%)
  other arithmetic  35.8 us (19%)
  local copies, waits for them, and re-layouts  24.5 us (13%)
  waiting for transfers between devices  14 us (7%)
  starting transfers between devices  8.08 us (4%)
    psum x1, blocking collectives, per_device(): lax.psum(jnp.sum(gradient_slice * gradient_slice), ('replica', 'shard'))  64.2 us
    pmax x1, blocking collectives, per_device(): absmax = lax.pmax(block_max(deltas), 'replica')  39.3 us
    unnamed x15, local copies, waits for them, and re-layouts  18.7 us
    broadcast_in_dim x1, other arithmetic, per_device(): encoded[None]  14.9 us
    all_to_all x1, waiting for transfers between devices, per_device(): lax.all_to_all(encoded[None], 'replica', split_axis=1, concat_axis=0, til...  14 us
    unnamed x2, other arithmetic  10.5 us
    all_to_all x1, starting transfers between devices, get_ports(): jax.lax.all_to_all(jnp.stack([a0 for _ in range(jax.lax.axis_size('replic...  4.34 us
  transfers between devices with their start and end apart: 2, of which 1 were waited for; matrix products, arithmetic and copies ran while one was open for 3% of the time, Pallas kernels for 0%

profile of v2, /device:TPU:0, one launch (start us, length us, event | category | flops | bytes accessed | tf_op | source)
XLA Modules:
  0.0 187.4 jit_solution(12963420851941670942)
XLA Ops:
  0.6 2.1 %abs_bitcast_fusion = f32[16,8,32,128]{3,1,2,0:T(8,128)S(1)} fusion(f32[128,4096]{1,0:T(8,128)} %param.3, bf16[1,128,4096]{2,1,0:T(8,128)(2,1)} %param.4), kind=kLoop, calls=%fused_computation.7 | loop fusion | flops 1572864 | bytes 5242880
  2.7 1.7 copy.11
  4.4 0.0 copy-start
  4.4 0.0 copy-start.2
  4.4 2.4 %reduce_max.9 = f32[128,32]{1,0:T(8,128)S(1)} reduce(f32[128,32,128]{2,1,0:T(8,128)} %bitcast.35, f32[]{:T(128)} %constant.9.clone.1), dimensions={2}, to_apply=%region_0.0 | reduce | flops 520192 | bytes 2113540 | tf_op jit(solution)/shard_map/reduce_max | solution.py:33
  6.8 39.3 %pmax.7 = f32[128,32]{1,0:T(8,128)S(1)} all-reduce(f32[128,32]{1,0:T(8,128)S(1)} %reduce_max.9), channel_id=1, replica_groups=mesh['replica'=8,'shard'=4] {'replica'}, use_global_device_ids=true, to_apply=%region_1.0 | all-reduce | flops 4096 | bytes 32768 | tf_op jit(solution)/shard_map/pmax | solution.py:45
  46.1 0.6 broadcast_in_dim.6
  46.7 0.0 copy-start.1
  46.8 1.3 copy-done.1
  48.1 0.0 copy-done
  48.1 0.0 copy-done.2
  48.1 14.9 %fusion.2 = bf16[1,128,4096]{2,1,0:T(8,128)(2,1)S(1)} fusion(f32[128,4096]{1,0:T(8,128)S(1)} %copy-done, bf16[1,128,4096]{2,1,0:T(8,128)(2,1)S(1)} %copy-done.2, f32[16,8,32,128]{3,2,1,0:T(8,128)S(1)} %bitcast.31), kind=kLoop, calls=%fused_computation.9 | loop fusion | flops 5767168 | bytes 6291456 | tf_op jit(solution)/shard_map/broadcast_in_dim | solution.py:48
  62.9 3.7 %copy.18 = bf16[1,128,4096]{2,0,1:T(2,128)(2,1)} copy(bf16[1,128,4096]{2,1,0:T(8,128)(2,1)S(1)} %fusion.2) | data formatting | bytes 2097152 | tf_op jit(solution)/shard_map/broadcast_in_dim | solution.py:48
  66.6 0.5 broadcast.29
  67.1 8.4 %reduce = bf16[128,4096]{1,0:T(8,128)(2,1)S(1)} reduce(bf16[128,1,4096]{2,1,0:T(2,128)(2,1)} %bitcast.34, bf16[]{:T(256)} %broadcast.29), dimensions={1}, to_apply=%bitcast.30.reduce_sub_computation | reduce | bytes 2097154
  75.5 1.6 reshape.28
  77.1 3.7 %all-to-all-start = ((bf16[8,2,32768]{2,1,0:T(2,128)(2,1)}), bf16[8,2,32768]{2,1,0:T(2,128)(2,1)S(1)}, u32[]{:S(2)}, u32[]{:S(2)}) async-start(bf16[8,2,32768]{2,1,0:T(2,128)(2,1)} %reshape.28), calls=%async_computation | async-start | bytes 2097152 | tf_op jit(solution)/shard_map/all_to_all | solution.py:48
  80.9 4.6 %copy.17 = f32[16,8,32,128]{3,1,2,0:T(8,128)} copy(f32[16,8,32,128]{3,2,1,0:T(8,128)} %bitcast.32) | data formatting | bytes 4194304
  85.4 14.0 %all-to-all-done = bf16[8,2,32768]{2,1,0:T(2,128)(2,1)S(1)} async-done(((bf16[8,2,32768]{2,1,0:T(2,128)(2,1)}), bf16[8,2,32768]{2,1,0:T(2,128)(2,1)S(1)}, u32[]{:S(2)}, u32[]{:S(2)}) %all-to-all-start) | async-done | bytes 1048608 | tf_op jit(solution)/shard_map/all_to_all | solution.py:48
  99.5 3.4 %reshape.29 = bf16[128,1,4096]{2,1,0:T(2,128)(2,1)} reshape(bf16[8,2,32768]{2,1,0:T(2,128)(2,1)S(1)} %all-to-all-done) | data formatting | bytes 2097152
  102.9 4.6 %copy.10 = f32[1,128,4096]{2,1,0:T(8,128)} copy(bf16[1,128,4096]{2,0,1:T(2,128)(2,1)} %bitcast.36) | data formatting | bytes 3145728
  107.5 1.7 reduce_sum.18
  109.2 1.6 multiply_reduce_fusion
  110.8 1.5 stack.2
  112.3 4.3 %all-to-all-start.1 = ((f32[8,16,4096]{2,1,0:T(8,128)}), f32[8,16,4096]{2,1,0:T(8,128)}, u32[]{:S(2)}, u32[]{:S(2)}) async-start(f32[8,16,4096]{2,1,0:T(8,128)} %stack.2), calls=%async_computation.1 | async-start | bytes 4194304 | tf_op jit(solution)/shard_map/all_to_all | solution.py:17
  116.7 0.7 copy.9
  117.4 64.2 %psum.7 = f32[]{:T(128)} all-reduce(f32[]{:T(128)} %get-tuple-element.11), channel_id=1, replica_groups=mesh['replica'=8,'shard'=4] {'replica','shard'}, use_global_device_ids=true, to_apply=%region_4.0 | all-reduce | flops 1 | bytes 8 | tf_op jit(solution)/shard_map/psum | solution.py:52
  182.3 0.0 all-to-all-done.1
  182.3 0.0 copy-start.3
  182.3 1.9 %broadcast_multiply_fusion = f32[8,16,4096]{2,1,0:T(8,128)S(1)} fusion(f32[8,16,4096]{2,1,0:T(8,128)} %all-to-all-done.1, f32[]{:T(128)S(6)} %min_shard_map.3), kind=kLoop, calls=%fused_computation.8 | loop fusion | flops 524288 | bytes 4194308 | tf_op jit(solution)/shard_map/mul | solution.py:57
  184.2 0.3 copy-done.3
  184.5 2.8 %fusion.1 = (f32[128,4096]{1,0:T(8,128)}, f32[128,4096]{1,0:T(8,128)}) fusion(f32[128,4096]{1,0:T(8,128)S(1)} %copy-done, f32[8,16,4096]{2,1,0:T(8,128)S(1)} %broadcast_multiply_fusion, f32[128,4096]{1,0:T(8,128)S(1)} %copy-done.3), kind=kLoop, calls=%fused_computation.5 | loop fusion | flops 3145728 | bytes 10485760 | tf_op jit(solution)/shard_map/sub | solution.py:59
  (1 shorter events, 0.0 us)
Async XLA Ops:
  4.4 43.6 %copy-start = (f32[128,4096]{1,0:T(8,128)S(1)}, f32[128,4096]{1,0:T(8,128)}, u32[]{:S(2)}) copy-start(f32[128,4096]{1,0:T(8,128)} %param.3) | copy-start | bytes 6291460
  4.4 43.6 %copy-start.2 = (bf16[1,128,4096]{2,1,0:T(8,128)(2,1)S(1)}, bf16[1,128,4096]{2,1,0:T(8,128)(2,1)}, u32[]{:S(2)}) copy-start(bf16[1,128,4096]{2,1,0:T(8,128)(2,1)} %param.4) | copy-start | bytes 3145732
  46.7 1.3 copy-start.1
  77.1 22.3 %all-to-all-start = ((bf16[8,2,32768]{2,1,0:T(2,128)(2,1)}), bf16[8,2,32768]{2,1,0:T(2,128)(2,1)S(1)}, u32[]{:S(2)}, u32[]{:S(2)}) async-start(bf16[8,2,32768]{2,1,0:T(2,128)(2,1)} %reshape.28), calls=%async_computation | async-start | bytes 2097152 | tf_op jit(solution)/shard_map/all_to_all | solution.py:48
  112.3 70.0 %all-to-all-start.1 = ((f32[8,16,4096]{2,1,0:T(8,128)}), f32[8,16,4096]{2,1,0:T(8,128)}, u32[]{:S(2)}, u32[]{:S(2)}) async-start(f32[8,16,4096]{2,1,0:T(8,128)} %stack.2), calls=%async_computation.1 | async-start | bytes 4194304 | tf_op jit(solution)/shard_map/all_to_all | solution.py:17
  182.3 2.2 %copy-start.3 = (f32[128,4096]{1,0:T(8,128)S(1)}, f32[128,4096]{1,0:T(8,128)}, u32[]{:S(2)}) copy-start(f32[128,4096]{1,0:T(8,128)} %param.5) | copy-start | bytes 6291460
